TPU v7x, 256 devices: a whole 4x4x8 slice. The times are simulated.
256 devices in a mesh: img: 16 (over y, x), row: 16 (over z, core).
Axes of the slice: x: 4, y: 4, z: 8, core: 2. Of those that a mesh axis runs over, the one named last changes fastest.
Arguments:
- latent: bfloat16 [1024, 128, 512], P(('img', 'row')), parts along dimension 0, may hold values from -8 to 8
- attn_gain: float32 [512], replicated, may hold values from 0.5 to 1.5
- attn_shift: float32 [512], replicated, may hold values from -3 to 3
- w_query: bfloat16 [512, 512], replicated, may hold values from -2 to 2
- w_key: bfloat16 [512, 512], replicated, may hold values from -2 to 2
- w_value: bfloat16 [512, 512], replicated, may hold values from -0.25 to 0.25
- w_out: bfloat16 [512, 512], replicated, may hold values from -0.25 to 0.25
- conv_gain: float32 [512], replicated, may hold values from 0.5 to 1.5
- conv_shift: float32 [512], replicated, may hold values from -3 to 3
- w_conv: bfloat16 [3, 3, 512, 512], replicated, may hold values from -0.09375 to 0.09375
- conv_bias: float32 [512], replicated, may hold values from -3 to 3
Outputs:
- encoded: bfloat16 [1024, 128, 512], P(('img', 'row')), parts along dimension 0
There are 16 independent parts, one for each index of `img`. A program takes and returns all parts, laid end to end along the dimension named above; an argument that names none is the same for every part. Nothing has to cross between parts.
All inputs are finite; a program needn't handle non-finite values.
Results may differ from a plain program's by a relative error of at most 0.011.
Values may be sent and summed in bfloat16 or wider, within the bound.
No kernel may reach another device: no remote copies, remote signals or barrier semaphores. Data moves between devices by JAX's collectives and lax.ppermute only.
A program may use at most 128 MiB of HBM per device.

v0:
```python
import jax
import jax.numpy as jnp
from jax import lax
from jax.sharding import PartitionSpec as P

C = 512
GROUPS = 32
W = 128
epsilon = 1e-06


def copy_for_each(shard, axis):
    copies = jnp.broadcast_to(shard, (lax.axis_size(axis), *shard.shape))
    return lax.all_to_all(copies, axis, split_axis=0, concat_axis=0, tiled=True)


def taken_together(shard, axis):
    return copy_for_each(shard, axis).sum(axis=0)


def together(arrays, axis):
    line, at, done = (jnp.concatenate([a.reshape(-1) for a in arrays]), 0, [])
    total = taken_together(line, axis)
    for a in arrays:
        done.append(total[at : at + a.size].reshape(a.shape))
        at += a.size
    return tuple(done)


def with_halo(cells, sides, width):
    for axis, dim in sides:
        count = lax.axis_size(axis)
        ends = count - 1
        head = lax.slice_in_dim(cells, 0, width, axis=dim)
        tail = lax.slice_in_dim(cells, cells.shape[dim] - width, cells.shape[dim], axis=dim)
        cells = jnp.concatenate(
            [
                lax.ppermute(tail, axis, [(i, (i + 1) % count) for i in range(ends)]),
                cells,
                lax.ppermute(head, axis, [((i + 1) % count, i) for i in range(ends)]),
            ],
            axis=dim,
        )
    return cells


def group_stats(grouped, count):
    first, second = together(
        (jnp.sum(grouped, axis=(0, 2)), jnp.sum(grouped * grouped, axis=(0, 2))), "row"
    )
    centre = first / count
    spread = second / count - centre * centre
    return (centre, spread)


def group_norm(field, gain, shift):
    grouped = field.reshape(field.shape[0], GROUPS, C // GROUPS)
    count = field.shape[0] * lax.axis_size("row") * (C // GROUPS)
    centre, spread = group_stats(grouped, count)
    normed = (grouped - centre[None, :, None]) * lax.rsqrt(spread + epsilon)[None, :, None]
    return normed.reshape(field.shape) * gain + shift


def attend(carry, key_piece, value_piece, queries):
    maxima, denominator, accumulated = carry
    scaling = 1.0 / jnp.sqrt(jnp.float32(C))
    scores = (
        jnp.einsum("qc,kc->qk", queries, key_piece, preferred_element_type=jnp.float32) * scaling
    )
    newest = jnp.maximum(maxima, jnp.max(scores, axis=1))
    expo = jnp.exp(scores - newest[:, None])
    denominator = jnp.sum(expo, axis=1)
    accumulated = jnp.dot(
        expo.astype(jnp.bfloat16), value_piece, preferred_element_type=jnp.float32
    )
    return (newest, denominator, accumulated)


def local(
    latent,
    attn_gain,
    attn_shift,
    w_query,
    w_key,
    w_value,
    w_out,
    conv_gain,
    conv_shift,
    w_conv,
    conv_bias,
):
    local_rows = latent.shape[0]
    positions = latent.reshape(local_rows * W, C)
    normed = group_norm(positions.astype(jnp.float32), attn_gain, attn_shift).astype(jnp.bfloat16)
    queries = jnp.dot(normed, w_query, preferred_element_type=jnp.float32).astype(jnp.bfloat16)
    count_rows = positions.shape[0]
    start_carry = (
        jnp.full((count_rows,), -1e30, jnp.float32),
        jnp.zeros((count_rows,), jnp.float32),
        jnp.zeros((count_rows, C), jnp.float32),
    )
    piece = lax.all_gather(normed, "row", axis=0, tiled=True)
    key_piece = jnp.dot(piece, w_key, preferred_element_type=jnp.float32).astype(jnp.bfloat16)
    value_piece = jnp.dot(piece, w_value, preferred_element_type=jnp.float32).astype(jnp.bfloat16)
    maxima, denominator, accumulated = attend(start_carry, key_piece, value_piece, queries)
    attended = (accumulated / denominator[:, None]).astype(jnp.bfloat16)
    hidden = (
        positions.astype(jnp.float32) + jnp.dot(attended, w_out, preferred_element_type=jnp.float32)
    ).astype(jnp.bfloat16)
    activated = jax.nn.silu(group_norm(hidden.astype(jnp.float32), conv_gain, conv_shift)).astype(
        jnp.bfloat16
    )
    activated = activated.reshape(local_rows, W, C)
    bordered = with_halo(activated, (("row", 0),), 1)
    padded = jnp.pad(bordered, ((0, 0), (1, 1), (0, 0)))
    convolved = jnp.zeros((local_rows * W, C), jnp.float32)
    for row_tap in range(3):
        for col_tap in range(3):
            window = padded[row_tap : row_tap + local_rows, col_tap : col_tap + W].reshape(
                local_rows * W, C
            )
            convolved = convolved + jnp.dot(
                window, w_conv[row_tap, col_tap], preferred_element_type=jnp.float32
            )
    encoded = hidden.astype(jnp.float32) + (convolved + conv_bias)
    return encoded.astype(jnp.bfloat16).reshape(local_rows, W, C)


def solution(mesh):
    in_specs = (P(("img", "row"), None, None), P(), P(), P(), P(), P(), P(), P(), P(), P(), P())
    out_specs = P(("img", "row"), None, None)
    return jax.shard_map(local, mesh=mesh, in_specs=in_specs, out_specs=out_specs, check_vma=False)
```

profile of v0, /device:TPU:1, one launch (start us, length us, event | category | flops | bytes accessed | tf_op | source)
XLA Modules:
  0.0 157.1 jit_solution(7887998248014053439)
XLA Ops:
  6.5 1.3 convert_reduce_fusion.1
  8.3 16.8 %all_to_all.12 = f32[16,1,64]{2,1,0:T(1,128)S(1)} all-to-all(f32[16,1,64]{2,1,0:T(1,128)S(1)} %broadcast_in_dim.6), channel_id=1, replica_groups=mesh['img'=16,'row'=16] {'row'}, dimensions={0} | all-to-all | bytes 8192 | tf_op jit(solution)/shard_map/all_to_all | solution.py:14
  25.5 2.1 %fusion.31 = bf16[512,512]{1,0:T(8,128)(2,1)} fusion(bf16[4,128,512]{2,1,0:T(8,128)(2,1)} %param.11, f32[512]{0:T(512)} %param.13, f32[512]{0:T(512)} %param.12, f32[512]{0:T(512)S(1)} %mul.69, f32[512]{0:T(512)S(1)} %sub.41), kind=kLoop, calls=%fused_computation.46 | loop fusion | flops 1572864 | bytes 1056768 | tf_op jit(solution)/shard_map/convert_element_type | solution.py:94
  27.6 1.6 %convolution_convert_fusion.2 = bf16[512,512]{1,0:T(8,128)(2,1)S(1)} fusion(bf16[512,512]{1,0:T(8,128)(2,1)} %fusion.31, bf16[512,512]{1,0:T(8,128)(2,1)} %param.14), kind=kOutput, calls=%fused_computation.28 | convolution fusion | flops 268697600 | bytes 1572864 | tf_op jit(solution)/shard_map/dot_general | solution.py:95
  29.2 51.1 %all-gather.2.cloned.1.call-done = bf16[8192,512]{1,0:T(8,128)(2,1)} async-done(((bf16[512,512]{1,0:T(8,128)(2,1)}), bf16[8192,512]{1,0:T(8,128)(2,1)}) %all-gather.2.cloned.1.call-update) | async-done | bytes 8388624 | tf_op jit(solution)/shard_map/all_gather | solution.py:102
  80.4 14.5 %multiply_reduce_fusion = (f32[512]{0:T(512)S(1)}, f32[512,8192]{1,0:T(8,128)}) fusion(bf16[512,512]{1,0:T(8,128)(2,1)S(1)} %convolution_convert_fusion.2, bf16[8192,512]{1,0:T(8,128)(2,1)} %all-gather.2.cloned.1.call-done, bf16[512,512]{1,0:T(8,128)(2,1)S(1)} %copy-done), kind=kOutput, calls=%fused_computation.1 | convolution fusion | flops 8602517504 | bytes 26216448 | tf_op jit(solution)/shard_map/qc,kc->qk/dot_general | solution.py:68
  94.9 8.7 %fusion = f32[512]{0:T(512)S(1)} fusion(f32[512,8192]{1,0:T(8,128)} %get-tuple-element.24, f32[512]{0:T(512)S(1)} %broadcast_maximum_fusion), kind=kLoop, calls=%fused_computation.2 | loop fusion | flops 12582400 | bytes 16781312 | tf_op jit(solution)/shard_map/reduce_sum | solution.py:72
  103.6 17.2 %fusion.15 = bf16[512,512]{1,0:T(8,128)(2,1)S(1)} fusion(bf16[8192,512]{1,0:T(8,128)(2,1)} %all-gather.2.cloned.1.call-done, bf16[512,512]{1,0:T(8,128)(2,1)S(1)} %copy-done.5, f32[512,8192]{1,0:T(8,128)} %get-tuple-element.24, f32[512]{0:T(512)S(1)} %broadcast_maximum_fusion, f32[512]{0:T(512)S(1)} %fusion), kind=kOutput, calls=%fused_computation.31 | convolution fusion | flops 8607236096 | bytes 26218496 | tf_op jit(solution)/shard_map/dot_general | solution.py:73
  120.8 0.5 convert_reduce_fusion
  122.0 11.4 %all_to_all.13 = f32[16,1,64]{2,1,0:T(1,128)S(1)} all-to-all(f32[16,1,64]{2,1,0:T(1,128)S(1)} %broadcast_in_dim.8), channel_id=1, replica_groups=mesh['img'=16,'row'=16] {'row'}, dimensions={0} | all-to-all | bytes 8192 | tf_op jit(solution)/shard_map/all_to_all | solution.py:14
  133.8 0.4 fusion.27
  134.2 2.7 %collective-permute-start = (bf16[1,128,512]{2,1,0:T(8,128)(2,1)S(1)}, bf16[1,128,512]{2,1,0:T(8,128)(2,1)S(1)}, u32[]{:S(2)}, u32[]{:S(2)}) collective-permute-start(bf16[1,128,512]{2,1,0:T(8,128)(2,1)S(1)} %get-tuple-element.17), channel_id=1, source_target_pairs={{0,1},{1,2},{2,3},{3,4},{4,5},{5,6},{6,7},{7,8},{8,9},{9,10},{10,1... | collective-permute-start | bytes 393224 | tf_op jit(solution)/shard_map/ppermute | solution.py:38
  137.0 1.9 %collective-permute-start.1 = (bf16[1,128,512]{2,1,0:T(8,128)(2,1)S(1)}, bf16[1,128,512]{2,1,0:T(8,128)(2,1)S(1)}, u32[]{:S(2)}, u32[]{:S(2)}) collective-permute-start(bf16[1,128,512]{2,1,0:T(8,128)(2,1)S(1)} %get-tuple-element.18), channel_id=1, source_target_pairs={{1,0},{2,1},{3,2},{4,3},{5,4},{6,5},{7,6},{8,7},{9,8},{10,9},{11,1... | collective-permute-start | bytes 393224 | tf_op jit(solution)/shard_map/ppermute | solution.py:40
  138.9 4.3 %collective-permute-done.1 = bf16[1,128,512]{2,1,0:T(8,128)(2,1)S(1)} collective-permute-done((bf16[1,128,512]{2,1,0:T(8,128)(2,1)S(1)}, bf16[1,128,512]{2,1,0:T(8,128)(2,1)S(1)}, u32[]{:S(2)}, u32[]{:S(2)}) %collective-permute-start.1) | collective-permute-done | bytes 131104 | tf_op jit(solution)/shard_map/ppermute | solution.py:40
  143.5 0.4 fusion.58
  143.9 1.7 %fusion.46 = f32[512,512]{1,0:T(8,128)S(1)} fusion(bf16[512,512]{1,0:T(8,128)(2,1)S(1)} %bitcast.82, bf16[3,3,512,512]{3,2,1,0:T(8,128)(2,1)} %param.20), kind=kOutput, calls=%fused_computation.65 | convolution fusion | flops 268435456 | bytes 2097152 | tf_op jit(solution)/shard_map/dot_general | solution.py:122
  145.8 0.4 convolution_add_fusion.6
  146.3 0.4 convolution_add_fusion.5
  146.7 0.4 convolution_add_fusion.4
  147.2 0.4 convolution_add_fusion.3
  147.6 0.4 fusion.37
  148.1 0.4 convolution_add_fusion.2
  148.5 0.4 convolution_add_fusion.1
  149.0 1.3 fusion.10
  (50 shorter events, 2.4 us)
Async XLA Ops:
  6.5 73.8 %copy-start = (bf16[512,512]{1,0:T(8,128)(2,1)S(1)}, bf16[512,512]{1,0:T(8,128)(2,1)}, u32[]{:S(2)}) copy-start(bf16[512,512]{1,0:T(8,128)(2,1)} %param.15) | copy-start | bytes 1572868
  6.5 73.8 %all-gather.2.cloned.1.call-start = ((), (), s32[]{:S(2)}) async-start(), calls=%async_computation.2 | async-start | bytes 8912896 | tf_op jit(solution)/shard_map/all_gather | solution.py:102
  94.9 8.7 %copy-start.5 = (bf16[512,512]{1,0:T(8,128)(2,1)S(1)}, bf16[512,512]{1,0:T(8,128)(2,1)}, u32[]{:S(2)}) copy-start(bf16[512,512]{1,0:T(8,128)(2,1)} %param.16) | copy-start | bytes 1572868
  103.6 17.2 %copy-start.1 = (bf16[4,128,512]{2,1,0:T(8,128)(2,1)S(1)}, bf16[4,128,512]{2,1,0:T(8,128)(2,1)}, u32[]{:S(2)}) copy-start(bf16[4,128,512]{2,1,0:T(8,128)(2,1)} %param.11) | copy-start | bytes 1572868
  103.6 17.2 %copy-start.6 = (bf16[512,512]{1,0:T(8,128)(2,1)S(1)}, bf16[512,512]{1,0:T(8,128)(2,1)}, u32[]{:S(2)}) copy-start(bf16[512,512]{1,0:T(8,128)(2,1)} %param.17) | copy-start | bytes 1572868
  103.6 30.2 %copy-start.2 = (f32[512]{0:T(512)S(1)}, f32[512]{0:T(512)}, u32[]{:S(2)}) copy-start(f32[512]{0:T(512)} %param.19) | copy-start | bytes 6148
  103.6 30.2 %copy-start.3 = (f32[512]{0:T(512)S(1)}, f32[512]{0:T(512)}, u32[]{:S(2)}) copy-start(f32[512]{0:T(512)} %param.18) | copy-start | bytes 6148
  120.8 24.9 %slice-start = ((s8[4718592]{0:T(1024)(128)(4,1)}), s8[524288]{0:T(1024)(128)(4,1)S(1)}, s32[]{:S(2)}) async-start(s8[4718592]{0:T(1024)(128)(4,1)} %bitcast.74), calls=%async_computation.3 | async-start | bytes 1048576
  134.2 4.7 %collective-permute-start = (bf16[1,128,512]{2,1,0:T(8,128)(2,1)S(1)}, bf16[1,128,512]{2,1,0:T(8,128)(2,1)S(1)}, u32[]{:S(2)}, u32[]{:S(2)}) collective-permute-start(bf16[1,128,512]{2,1,0:T(8,128)(2,1)S(1)} %get-tuple-element.17), channel_id=1, source_target_pairs={{0,1},{1,2},{2,3},{3,4},{4,5},{5,6},{6,7},{7,8},{8,9},{9,10},{10,1... | collective-permute-start | bytes 393224 | tf_op jit(solution)/shard_map/ppermute | solution.py:38
  137.0 6.3 %collective-permute-start.1 = (bf16[1,128,512]{2,1,0:T(8,128)(2,1)S(1)}, bf16[1,128,512]{2,1,0:T(8,128)(2,1)S(1)}, u32[]{:S(2)}, u32[]{:S(2)}) collective-permute-start(bf16[1,128,512]{2,1,0:T(8,128)(2,1)S(1)} %get-tuple-element.18), channel_id=1, source_target_pairs={{1,0},{2,1},{3,2},{4,3},{5,4},{6,5},{7,6},{8,7},{9,8},{10,9},{11,1... | collective-permute-start | bytes 393224 | tf_op jit(solution)/shard_map/ppermute | solution.py:40
  143.5 2.3 %slice-start.1 = ((s8[4718592]{0:T(1024)(128)(4,1)}), s8[4194304]{0:T(1024)(128)(4,1)S(1)}, s32[]{:S(2)}) async-start(s8[4718592]{0:T(1024)(128)(4,1)} %bitcast.74), calls=%async_computation.4 | async-start | bytes 8388608
  146.3 2.7 %copy-start.4 = (f32[512]{0:T(512)S(1)}, f32[512]{0:T(512)}, u32[]{:S(2)}) copy-start(f32[512]{0:T(512)} %param.21) | copy-start | bytes 6148
Sparse Core Ops, SparseCore 0:
  27.7 52.6 all-gather.1
where the time goes:
time: 157 us
  waiting for transfers between devices  55.5 us (35%)
  matrix products  39.9 us (25%)
  blocking collectives  28.2 us (18%)
  other arithmetic  13.7 us (9%)
  between operations  13.6 us (9%)
  starting transfers between devices  4.64 us (3%)
    all_gather x1, waiting for transfers between devices, local(): piece = lax.all_gather(normed, 'row', axis=0, tiled=True)  51.1 us
    all_to_all x2, blocking collectives, copy_for_each(): return lax.all_to_all(copies, axis, split_axis=0, concat_axis=0, tiled=True)  28.2 us
    dot_general x1, matrix products, attend(): jnp.dot(expo.astype(jnp.bfloat16), value_piece, preferred_element_type=jn...  17.2 us
    dot_general x1, matrix products, attend(): jnp.einsum('qc,kc->qk', queries, key_piece, preferred_element_type=jnp.fl...  14.5 us
    reduce_sum x1, other arithmetic, attend(): denominator = jnp.sum(expo, axis=1)  8.68 us
    dot_general x9, matrix products, local(): jnp.dot(window, w_conv[row_tap, col_tap], preferred_element_type=jnp.floa...  6.07 us
    ppermute x1, waiting for transfers between devices, with_halo(): lax.ppermute(head, axis, [((i + 1) % count, i) for i in range(ends)])  4.35 us
  transfers between devices with their start and end apart: 3, of which 2 were waited for; matrix products, arithmetic and copies ran while one was open for 1% of the time, Pallas kernels for 0%

commit v1 on v0

--- a/solution.py
+++ b/solution.py
@@ -99,7 +99,16 @@
         jnp.zeros((count_rows,), jnp.float32),
         jnp.zeros((count_rows, C), jnp.float32),
     )
-    piece = lax.all_gather(normed, "row", axis=0, tiled=True)
+    ways = lax.axis_size("row")
+    up = [(d, (d + 1) % ways) for d in range(ways)]
+    down = [(d, (d - 1) % ways) for d in range(ways)]
+    earlier, later = ([normed], [normed])
+    for _ in range(ways // 2):
+        earlier.append(lax.ppermute(earlier[-1], "row", up))
+    for _ in range((ways - 1) // 2):
+        later.append(lax.ppermute(later[-1], "row", down))
+    line_2 = jnp.concatenate([*earlier[::-1], *later[1:]], axis=0)
+    piece = jnp.roll(line_2, (lax.axis_index("row") - ways // 2) * normed.shape[0], axis=0)
     key_piece = jnp.dot(piece, w_key, preferred_element_type=jnp.float32).astype(jnp.bfloat16)
     value_piece = jnp.dot(piece, w_value, preferred_element_type=jnp.float32).astype(jnp.bfloat16)
     maxima, denominator, accumulated = attend(start_carry, key_piece, value_piece, queries)

time: 157 us -> 208 us (1.32)
  starting transfers between devices: 4.64 us -> 47.3 us
  local copies, waits for them, and re-layouts: 1.52 us -> 43.8 us
  waiting for transfers between devices: 55.5 us -> 30.4 us
  between operations: 13.6 us -> 0.33 us
  blocking collectives: 28.2 us -> 33.9 us
    all_gather x1 -> x0, waiting for transfers between devices: 51.1 us -> none  [local(): piece = lax.all_gather(normed, 'row', axis=0, tiled=True)]
    ppermute x0 -> x15, starting transfers between devices: none -> 42.7 us  [the longest x7 28.1 us: local(): later.append(lax.ppermute(later[-1], 'row', down))]
    unnamed x18 -> x73, local copies, waits for them, and re-layouts: 0.16 us -> 41.6 us
    ppermute x0 -> x15, waiting for transfers between devices: none -> 26 us  [the longest x8 20.5 us: local(): earlier.append(lax.ppermute(earlier[-1], 'row', up))]
    all_to_all x2, blocking collectives: 28.2 us -> 33.9 us  [copy_for_each(): return lax.all_to_all(copies, axis, split_axis=0, concat_axis=0, tiled=True)]
    dot_general x1, matrix products: 17.2 us -> 14.2 us  [attend(): jnp.dot(expo.astype(jnp.bfloat16), value_piece, preferred_element_type=jn...]
  transfers between devices with their start and end apart: 3 -> 17, of which waited for: 2 -> 14; matrix products, arithmetic and copies ran while one was open for 1% -> 12% of each run, Pallas kernels for 0% -> 0%
where the time goes in v1:
time: 208 us
  starting transfers between devices  47.3 us (23%)
  local copies, waits for them, and re-layouts  43.8 us (21%)
  matrix products  39 us (19%)
  blocking collectives  33.9 us (16%)
  waiting for transfers between devices  30.4 us (15%)
  other arithmetic  12.7 us (6%)
    unnamed x73, local copies, waits for them, and re-layouts  41.6 us
    all_to_all x2, blocking collectives, copy_for_each(): return lax.all_to_all(copies, axis, split_axis=0, concat_axis=0, tiled=True)  33.9 us
    ppermute x7, starting transfers between devices, local(): later.append(lax.ppermute(later[-1], 'row', down))  28.1 us
    ppermute x8, waiting for transfers between devices, local(): earlier.append(lax.ppermute(earlier[-1], 'row', up))  20.5 us
    dot_general x1, matrix products, attend(): jnp.einsum('qc,kc->qk', queries, key_piece, preferred_element_type=jnp.fl...  14.7 us
    ppermute x8, starting transfers between devices, local(): earlier.append(lax.ppermute(earlier[-1], 'row', up))  14.6 us
    dot_general x1, matrix products, attend(): jnp.dot(expo.astype(jnp.bfloat16), value_piece, preferred_element_type=jn...  14.2 us
    reduce_sum x1, other arithmetic, attend(): denominator = jnp.sum(expo, axis=1)  8.67 us
  transfers between devices with their start and end apart: 17, of which 14 were waited for; matrix products, arithmetic and copies ran while one was open for 12% of the time, Pallas kernels for 0%

profile of v1, /device:TPU:1, one launch (start us, length us, event | category | flops | bytes accessed | tf_op | source)
XLA Modules:
  0.0 207.5 jit_solution(2291904518519642536)
XLA Ops:
  1.8 16.8 %all_to_all.12 = f32[16,1,64]{2,1,0:T(1,128)S(1)} all-to-all(f32[16,1,64]{2,1,0:T(1,128)S(1)} %broadcast_in_dim.6), channel_id=1, replica_groups=mesh['img'=16,'row'=16] {'row'}, dimensions={0} | all-to-all | bytes 8192 | tf_op jit(solution)/shard_map/all_to_all | solution.py:14
  21.1 6.1 %collective-permute-done = bf16[512,512]{1,0:T(8,128)(2,1)S(1)} collective-permute-done((bf16[512,512]{1,0:T(8,128)(2,1)S(1)}, bf16[512,512]{1,0:T(8,128)(2,1)S(1)}, u32[]{:S(2)}, u32[]{:S(2)}) %collective-permute-start) | collective-permute-done | bytes 524320 | tf_op jit(solution)/shard_map/ppermute | solution.py:107
  27.2 2.5 %collective-permute-start.1 = (bf16[512,512]{1,0:T(8,128)(2,1)S(1)}, bf16[512,512]{1,0:T(8,128)(2,1)S(1)}, u32[]{:S(2)}, u32[]{:S(2)}) collective-permute-start(bf16[512,512]{1,0:T(8,128)(2,1)S(1)} %collective-permute-done), channel_id=1, source_target_pairs={{0,1},{1,2},{2,3},{3,4},{4,5},{5,6},{6,7},{7,8},{8,9},{9,10},{10,1... | collective-permute-start | bytes 1572872 | tf_op jit(solution)/shard_map/ppermute | solution.py:107
  30.7 5.1 %collective-permute-done.1 = bf16[512,512]{1,0:T(8,128)(2,1)S(1)} collective-permute-done((bf16[512,512]{1,0:T(8,128)(2,1)S(1)}, bf16[512,512]{1,0:T(8,128)(2,1)S(1)}, u32[]{:S(2)}, u32[]{:S(2)}) %collective-permute-start.1) | collective-permute-done | bytes 524320 | tf_op jit(solution)/shard_map/ppermute | solution.py:107
  35.8 2.5 %collective-permute-start.2 = (bf16[512,512]{1,0:T(8,128)(2,1)S(1)}, bf16[512,512]{1,0:T(8,128)(2,1)S(1)}, u32[]{:S(2)}, u32[]{:S(2)}) collective-permute-start(bf16[512,512]{1,0:T(8,128)(2,1)S(1)} %collective-permute-done.1), channel_id=1, source_target_pairs={{0,1},{1,2},{2,3},{3,4},{4,5},{5,6},{6,7},{7,8},{8,9},{9,10},{10,1... | collective-permute-start | bytes 1572872 | tf_op jit(solution)/shard_map/ppermute | solution.py:107
  38.6 2.0 collective-permute-start.9
  40.6 3.9 %collective-permute-done.2 = bf16[512,512]{1,0:T(8,128)(2,1)S(1)} collective-permute-done((bf16[512,512]{1,0:T(8,128)(2,1)S(1)}, bf16[512,512]{1,0:T(8,128)(2,1)S(1)}, u32[]{:S(2)}, u32[]{:S(2)}) %collective-permute-start.2) | collective-permute-done | bytes 524320 | tf_op jit(solution)/shard_map/ppermute | solution.py:107
  44.4 2.5 %collective-permute-start.3 = (bf16[512,512]{1,0:T(8,128)(2,1)S(1)}, bf16[512,512]{1,0:T(8,128)(2,1)S(1)}, u32[]{:S(2)}, u32[]{:S(2)}) collective-permute-start(bf16[512,512]{1,0:T(8,128)(2,1)S(1)} %collective-permute-done.2), channel_id=1, source_target_pairs={{0,1},{1,2},{2,3},{3,4},{4,5},{5,6},{6,7},{7,8},{8,9},{9,10},{10,1... | collective-permute-start | bytes 1572872 | tf_op jit(solution)/shard_map/ppermute | solution.py:107
  47.5 2.9 %collective-permute-start.10 = (bf16[512,512]{1,0:T(8,128)(2,1)S(1)}, bf16[512,512]{1,0:T(8,128)(2,1)S(1)}, u32[]{:S(2)}, u32[]{:S(2)}) collective-permute-start(bf16[512,512]{1,0:T(8,128)(2,1)S(1)} %collective-permute-done.9), channel_id=1, source_target_pairs={{0,15},{1,0},{2,1},{3,2},{4,3},{5,4},{6,5},{7,6},{8,7},{9,8},{10,9... | collective-permute-start | bytes 1572872 | tf_op jit(solution)/shard_map/ppermute | solution.py:109
  50.4 2.6 %collective-permute-done.3 = bf16[512,512]{1,0:T(8,128)(2,1)S(1)} collective-permute-done((bf16[512,512]{1,0:T(8,128)(2,1)S(1)}, bf16[512,512]{1,0:T(8,128)(2,1)S(1)}, u32[]{:S(2)}, u32[]{:S(2)}) %collective-permute-start.3) | collective-permute-done | bytes 524320 | tf_op jit(solution)/shard_map/ppermute | solution.py:107
  53.0 2.5 %collective-permute-start.4 = (bf16[512,512]{1,0:T(8,128)(2,1)S(1)}, bf16[512,512]{1,0:T(8,128)(2,1)S(1)}, u32[]{:S(2)}, u32[]{:S(2)}) collective-permute-start(bf16[512,512]{1,0:T(8,128)(2,1)S(1)} %collective-permute-done.3), channel_id=1, source_target_pairs={{0,1},{1,2},{2,3},{3,4},{4,5},{5,6},{6,7},{7,8},{8,9},{9,10},{10,1... | collective-permute-start | bytes 1572872 | tf_op jit(solution)/shard_map/ppermute | solution.py:107
  56.4 3.8 %collective-permute-start.11 = (bf16[512,512]{1,0:T(8,128)(2,1)S(1)}, bf16[512,512]{1,0:T(8,128)(2,1)S(1)}, u32[]{:S(2)}, u32[]{:S(2)}) collective-permute-start(bf16[512,512]{1,0:T(8,128)(2,1)S(1)} %collective-permute-done.10), channel_id=1, source_target_pairs={{0,15},{1,0},{2,1},{3,2},{4,3},{5,4},{6,5},{7,6},{8,7},{9,8},{10,9... | collective-permute-start | bytes 1572872 | tf_op jit(solution)/shard_map/ppermute | solution.py:109
  61.6 2.5 %collective-permute-start.5 = (bf16[512,512]{1,0:T(8,128)(2,1)S(1)}, bf16[512,512]{1,0:T(8,128)(2,1)S(1)}, u32[]{:S(2)}, u32[]{:S(2)}) collective-permute-start(bf16[512,512]{1,0:T(8,128)(2,1)S(1)} %collective-permute-done.4), channel_id=1, source_target_pairs={{0,1},{1,2},{2,3},{3,4},{4,5},{5,6},{6,7},{7,8},{8,9},{9,10},{10,1... | collective-permute-start | bytes 1572872 | tf_op jit(solution)/shard_map/ppermute | solution.py:107
  66.1 4.8 %collective-permute-start.12 = (bf16[512,512]{1,0:T(8,128)(2,1)S(1)}, bf16[512,512]{1,0:T(8,128)(2,1)}, u32[]{:S(2)}, u32[]{:S(2)}) collective-permute-start(bf16[512,512]{1,0:T(8,128)(2,1)S(1)} %collective-permute-done.11), channel_id=1, source_target_pairs={{0,15},{1,0},{2,1},{3,2},{4,3},{5,4},{6,5},{7,6},{8,7},{9,8},{10,9... | collective-permute-start | bytes 1572872 | tf_op jit(solution)/shard_map/ppermute | solution.py:109
  72.7 2.3 %collective-permute-done.12 = bf16[512,512]{1,0:T(8,128)(2,1)} collective-permute-done((bf16[512,512]{1,0:T(8,128)(2,1)S(1)}, bf16[512,512]{1,0:T(8,128)(2,1)}, u32[]{:S(2)}, u32[]{:S(2)}) %collective-permute-start.12) | collective-permute-done | bytes 524320 | tf_op jit(solution)/shard_map/ppermute | solution.py:109
  75.0 5.5 %collective-permute-start.13 = (bf16[512,512]{1,0:T(8,128)(2,1)}, bf16[512,512]{1,0:T(8,128)(2,1)}, u32[]{:S(2)}, u32[]{:S(2)}) collective-permute-start(bf16[512,512]{1,0:T(8,128)(2,1)} %collective-permute-done.12), channel_id=1, source_target_pairs={{0,15},{1,0},{2,1},{3,2},{4,3},{5,4},{6,5},{7,6},{8,7},{9,8},{10,9... | collective-permute-start | bytes 1572872 | tf_op jit(solution)/shard_map/ppermute | solution.py:109
  81.5 2.4 %convolution_convert_fusion.2 = bf16[512,512]{1,0:T(8,128)(2,1)} fusion(bf16[512,512]{1,0:T(8,128)(2,1)S(1)} %fusion.41, bf16[512,512]{1,0:T(8,128)(2,1)} %param.14), kind=kOutput, calls=%fused_computation.30 | convolution fusion | flops 268697600 | bytes 1572864 | tf_op jit(solution)/shard_map/dot_general | solution.py:95
  84.2 8.0 %collective-permute-start.14 = (bf16[512,512]{1,0:T(8,128)(2,1)}, bf16[512,512]{1,0:T(8,128)(2,1)S(1)}, u32[]{:S(2)}, u32[]{:S(2)}) collective-permute-start(bf16[512,512]{1,0:T(8,128)(2,1)} %collective-permute-done.13), channel_id=1, source_target_pairs={{0,15},{1,0},{2,1},{3,2},{4,3},{5,4},{6,5},{7,6},{8,7},{9,8},{10,9... | collective-permute-start | bytes 1572872 | tf_op jit(solution)/shard_map/ppermute | solution.py:109
  133.8 14.7 %multiply_reduce_fusion = (f32[512]{0:T(512)S(1)}, f32[512,8192]{1,0:T(8,128)}) fusion(bf16[512,512]{1,0:T(8,128)(2,1)} %convolution_convert_fusion.2, bf16[512,512]{1,0:T(8,128)(2,1)S(1)} %copy-done, bf16[16384,512]{1,0:T(8,128)(2,1)} %constant_dynamic-update-slice_fusion, s32[]{:T(128)S(6)} %select_n.14), kind=kOutput, calls=%fused_computation.1 | convolution fusion | flops 8602517504 | bytes 26216452 | tf_op jit(solution)/shard_map/qc,kc->qk/dot_general | solution.py:68
  148.6 8.7 %fusion = f32[512]{0:T(512)S(1)} fusion(f32[512,8192]{1,0:T(8,128)} %get-tuple-element.24, f32[512]{0:T(512)S(1)} %broadcast_maximum_fusion), kind=kLoop, calls=%fused_computation.2 | loop fusion | flops 12582400 | bytes 16781312 | tf_op jit(solution)/shard_map/reduce_sum | solution.py:72
  157.3 14.2 %fusion.23 = bf16[512,512]{1,0:T(8,128)(2,1)S(1)} fusion(bf16[512,512]{1,0:T(8,128)(2,1)S(1)} %copy-done.17, bf16[16384,512]{1,0:T(8,128)(2,1)} %constant_dynamic-update-slice_fusion, s32[]{:T(128)S(6)} %select_n.14, f32[512,8192]{1,0:T(8,128)} %get-tuple-element.24, f32[512]{0:T(512)S(1)} %broadcast_maximum_fusion, f32[512]{0:T(512)S(1)} %fusion), kind=kOutput, calls=%fused_computation.33 | convolution fusion | flops 8607236096 | bytes 26218500 | tf_op jit(solution)/shard_map/dot_general | solution.py:73
  172.6 17.1 %all_to_all.13 = f32[16,1,64]{2,1,0:T(1,128)S(1)} all-to-all(f32[16,1,64]{2,1,0:T(1,128)S(1)} %broadcast_in_dim.8), channel_id=1, replica_groups=mesh['img'=16,'row'=16] {'row'}, dimensions={0} | all-to-all | bytes 8192 | tf_op jit(solution)/shard_map/all_to_all | solution.py:14
  190.5 2.7 %collective-permute-start.15 = (bf16[1,128,512]{2,1,0:T(8,128)(2,1)S(1)}, bf16[1,128,512]{2,1,0:T(8,128)(2,1)S(1)}, u32[]{:S(2)}, u32[]{:S(2)}) collective-permute-start(bf16[1,128,512]{2,1,0:T(8,128)(2,1)S(1)} %get-tuple-element.17), channel_id=1, source_target_pairs={{0,1},{1,2},{2,3},{3,4},{4,5},{5,6},{6,7},{7,8},{8,9},{9,10},{10,1... | collective-permute-start | bytes 393224 | tf_op jit(solution)/shard_map/ppermute | solution.py:38
  195.2 4.3 %collective-permute-done.16 = bf16[1,128,512]{2,1,0:T(8,128)(2,1)S(1)} collective-permute-done((bf16[1,128,512]{2,1,0:T(8,128)(2,1)S(1)}, bf16[1,128,512]{2,1,0:T(8,128)(2,1)S(1)}, u32[]{:S(2)}, u32[]{:S(2)}) %collective-permute-start.16) | collective-permute-done | bytes 131104 | tf_op jit(solution)/shard_map/ppermute | solution.py:40
  (133 shorter events, 66.7 us)
Async XLA Ops:
  0.0 133.8 %copy-start = (bf16[512,512]{1,0:T(8,128)(2,1)S(1)}, bf16[512,512]{1,0:T(8,128)(2,1)}, u32[]{:S(2)}) copy-start(bf16[512,512]{1,0:T(8,128)(2,1)} %param.15) | copy-start | bytes 1572868
  20.2 7.0 %collective-permute-start = (bf16[512,512]{1,0:T(8,128)(2,1)S(1)}, bf16[512,512]{1,0:T(8,128)(2,1)S(1)}, u32[]{:S(2)}, u32[]{:S(2)}) collective-permute-start(bf16[512,512]{1,0:T(8,128)(2,1)S(1)} %fusion.41), channel_id=1, source_target_pairs={{0,1},{1,2},{2,3},{3,4},{4,5},{5,6},{6,7},{7,8},{8,9},{9,10},{10,1... | collective-permute-start | bytes 1572872 | tf_op jit(solution)/shard_map/ppermute | solution.py:107
  27.2 8.6 %collective-permute-start.1 = (bf16[512,512]{1,0:T(8,128)(2,1)S(1)}, bf16[512,512]{1,0:T(8,128)(2,1)S(1)}, u32[]{:S(2)}, u32[]{:S(2)}) collective-permute-start(bf16[512,512]{1,0:T(8,128)(2,1)S(1)} %collective-permute-done), channel_id=1, source_target_pairs={{0,1},{1,2},{2,3},{3,4},{4,5},{5,6},{6,7},{7,8},{8,9},{9,10},{10,1... | collective-permute-start | bytes 1572872 | tf_op jit(solution)/shard_map/ppermute | solution.py:107
  29.7 8.9 %collective-permute-start.8 = (bf16[512,512]{1,0:T(8,128)(2,1)S(1)}, bf16[512,512]{1,0:T(8,128)(2,1)S(1)}, u32[]{:S(2)}, u32[]{:S(2)}) collective-permute-start(bf16[512,512]{1,0:T(8,128)(2,1)S(1)} %fusion.41), channel_id=1, source_target_pairs={{0,15},{1,0},{2,1},{3,2},{4,3},{5,4},{6,5},{7,6},{8,7},{9,8},{10,9... | collective-permute-start | bytes 1572872 | tf_op jit(solution)/shard_map/ppermute | solution.py:109
  35.8 8.6 %collective-permute-start.2 = (bf16[512,512]{1,0:T(8,128)(2,1)S(1)}, bf16[512,512]{1,0:T(8,128)(2,1)S(1)}, u32[]{:S(2)}, u32[]{:S(2)}) collective-permute-start(bf16[512,512]{1,0:T(8,128)(2,1)S(1)} %collective-permute-done.1), channel_id=1, source_target_pairs={{0,1},{1,2},{2,3},{3,4},{4,5},{5,6},{6,7},{7,8},{8,9},{9,10},{10,1... | collective-permute-start | bytes 1572872 | tf_op jit(solution)/shard_map/ppermute | solution.py:107
  38.6 8.9 %collective-permute-start.9 = (bf16[512,512]{1,0:T(8,128)(2,1)S(1)}, bf16[512,512]{1,0:T(8,128)(2,1)S(1)}, u32[]{:S(2)}, u32[]{:S(2)}) collective-permute-start(bf16[512,512]{1,0:T(8,128)(2,1)S(1)} %collective-permute-done.8), channel_id=1, source_target_pairs={{0,15},{1,0},{2,1},{3,2},{4,3},{5,4},{6,5},{7,6},{8,7},{9,8},{10,9... | collective-permute-start | bytes 1572872 | tf_op jit(solution)/shard_map/ppermute | solution.py:109
  44.4 8.6 %collective-permute-start.3 = (bf16[512,512]{1,0:T(8,128)(2,1)S(1)}, bf16[512,512]{1,0:T(8,128)(2,1)S(1)}, u32[]{:S(2)}, u32[]{:S(2)}) collective-permute-start(bf16[512,512]{1,0:T(8,128)(2,1)S(1)} %collective-permute-done.2), channel_id=1, source_target_pairs={{0,1},{1,2},{2,3},{3,4},{4,5},{5,6},{6,7},{7,8},{8,9},{9,10},{10,1... | collective-permute-start | bytes 1572872 | tf_op jit(solution)/shard_map/ppermute | solution.py:107
  47.5 8.9 %collective-permute-start.10 = (bf16[512,512]{1,0:T(8,128)(2,1)S(1)}, bf16[512,512]{1,0:T(8,128)(2,1)S(1)}, u32[]{:S(2)}, u32[]{:S(2)}) collective-permute-start(bf16[512,512]{1,0:T(8,128)(2,1)S(1)} %collective-permute-done.9), channel_id=1, source_target_pairs={{0,15},{1,0},{2,1},{3,2},{4,3},{5,4},{6,5},{7,6},{8,7},{9,8},{10,9... | collective-permute-start | bytes 1572872 | tf_op jit(solution)/shard_map/ppermute | solution.py:109
  53.0 8.6 %collective-permute-start.4 = (bf16[512,512]{1,0:T(8,128)(2,1)S(1)}, bf16[512,512]{1,0:T(8,128)(2,1)S(1)}, u32[]{:S(2)}, u32[]{:S(2)}) collective-permute-start(bf16[512,512]{1,0:T(8,128)(2,1)S(1)} %collective-permute-done.3), channel_id=1, source_target_pairs={{0,1},{1,2},{2,3},{3,4},{4,5},{5,6},{6,7},{7,8},{8,9},{9,10},{10,1... | collective-permute-start | bytes 1572872 | tf_op jit(solution)/shard_map/ppermute | solution.py:107
  56.4 8.9 %collective-permute-start.11 = (bf16[512,512]{1,0:T(8,128)(2,1)S(1)}, bf16[512,512]{1,0:T(8,128)(2,1)S(1)}, u32[]{:S(2)}, u32[]{:S(2)}) collective-permute-start(bf16[512,512]{1,0:T(8,128)(2,1)S(1)} %collective-permute-done.10), channel_id=1, source_target_pairs={{0,15},{1,0},{2,1},{3,2},{4,3},{5,4},{6,5},{7,6},{8,7},{9,8},{10,9... | collective-permute-start | bytes 1572872 | tf_op jit(solution)/shard_map/ppermute | solution.py:109
  61.6 9.8 %collective-permute-start.5 = (bf16[512,512]{1,0:T(8,128)(2,1)S(1)}, bf16[512,512]{1,0:T(8,128)(2,1)S(1)}, u32[]{:S(2)}, u32[]{:S(2)}) collective-permute-start(bf16[512,512]{1,0:T(8,128)(2,1)S(1)} %collective-permute-done.4), channel_id=1, source_target_pairs={{0,1},{1,2},{2,3},{3,4},{4,5},{5,6},{6,7},{7,8},{8,9},{9,10},{10,1... | collective-permute-start | bytes 1572872 | tf_op jit(solution)/shard_map/ppermute | solution.py:107
  66.1 8.9 %collective-permute-start.12 = (bf16[512,512]{1,0:T(8,128)(2,1)S(1)}, bf16[512,512]{1,0:T(8,128)(2,1)}, u32[]{:S(2)}, u32[]{:S(2)}) collective-permute-start(bf16[512,512]{1,0:T(8,128)(2,1)S(1)} %collective-permute-done.11), channel_id=1, source_target_pairs={{0,15},{1,0},{2,1},{3,2},{4,3},{5,4},{6,5},{7,6},{8,7},{9,8},{10,9... | collective-permute-start | bytes 1572872 | tf_op jit(solution)/shard_map/ppermute | solution.py:109
  71.4 9.9 %collective-permute-start.6 = (bf16[512,512]{1,0:T(8,128)(2,1)S(1)}, bf16[512,512]{1,0:T(8,128)(2,1)}, u32[]{:S(2)}, u32[]{:S(2)}) collective-permute-start(bf16[512,512]{1,0:T(8,128)(2,1)S(1)} %collective-permute-done.5), channel_id=1, source_target_pairs={{0,1},{1,2},{2,3},{3,4},{4,5},{5,6},{6,7},{7,8},{8,9},{9,10},{10,1... | collective-permute-start | bytes 1572872 | tf_op jit(solution)/shard_map/ppermute | solution.py:107
  75.0 9.2 %collective-permute-start.13 = (bf16[512,512]{1,0:T(8,128)(2,1)}, bf16[512,512]{1,0:T(8,128)(2,1)}, u32[]{:S(2)}, u32[]{:S(2)}) collective-permute-start(bf16[512,512]{1,0:T(8,128)(2,1)} %collective-permute-done.12), channel_id=1, source_target_pairs={{0,15},{1,0},{2,1},{3,2},{4,3},{5,4},{6,5},{7,6},{8,7},{9,8},{10,9... | collective-permute-start | bytes 1572872 | tf_op jit(solution)/shard_map/ppermute | solution.py:109
  81.4 10.9 %collective-permute-start.7 = (bf16[512,512]{1,0:T(8,128)(2,1)}, bf16[512,512]{1,0:T(8,128)(2,1)}, u32[]{:S(2)}, u32[]{:S(2)}) collective-permute-start(bf16[512,512]{1,0:T(8,128)(2,1)} %collective-permute-done.6), channel_id=1, source_target_pairs={{0,1},{1,2},{2,3},{3,4},{4,5},{5,6},{6,7},{7,8},{8,9},{9,10},{10,1... | collective-permute-start | bytes 1572872 | tf_op jit(solution)/shard_map/ppermute | solution.py:107
  81.4 38.5 %copy-start.13 = (bf16[512,512]{1,0:T(8,128)(2,1)S(1)}, bf16[512,512]{1,0:T(8,128)(2,1)}, u32[]{:S(2)}) copy-start(bf16[512,512]{1,0:T(8,128)(2,1)} %copy-done.12) | copy-start | bytes 1572868
  81.4 39.3 %copy-start.11 = (bf16[512,512]{1,0:T(8,128)(2,1)S(1)}, bf16[512,512]{1,0:T(8,128)(2,1)}, u32[]{:S(2)}) copy-start(bf16[512,512]{1,0:T(8,128)(2,1)} %copy-done.10) | copy-start | bytes 1572868
  81.4 40.2 %copy-start.9 = (bf16[512,512]{1,0:T(8,128)(2,1)S(1)}, bf16[512,512]{1,0:T(8,128)(2,1)}, u32[]{:S(2)}) copy-start(bf16[512,512]{1,0:T(8,128)(2,1)} %copy-done.8) | copy-start | bytes 1572868
  81.4 41.0 %copy-start.3 = (bf16[512,512]{1,0:T(8,128)(2,1)S(1)}, bf16[512,512]{1,0:T(8,128)(2,1)}, u32[]{:S(2)}) copy-start(bf16[512,512]{1,0:T(8,128)(2,1)} %copy-done.2) | copy-start | bytes 1572868
  81.4 46.1 %copy-start.5 = (bf16[512,512]{1,0:T(8,128)(2,1)S(1)}, bf16[512,512]{1,0:T(8,128)(2,1)}, u32[]{:S(2)}) copy-start(bf16[512,512]{1,0:T(8,128)(2,1)} %copy-done.4) | copy-start | bytes 1572868
  81.5 46.9 %copy-start.7 = (bf16[512,512]{1,0:T(8,128)(2,1)S(1)}, bf16[512,512]{1,0:T(8,128)(2,1)}, u32[]{:S(2)}) copy-start(bf16[512,512]{1,0:T(8,128)(2,1)} %copy-done.6) | copy-start | bytes 1572868
  84.2 31.0 %collective-permute-start.14 = (bf16[512,512]{1,0:T(8,128)(2,1)}, bf16[512,512]{1,0:T(8,128)(2,1)S(1)}, u32[]{:S(2)}, u32[]{:S(2)}) collective-permute-start(bf16[512,512]{1,0:T(8,128)(2,1)} %collective-permute-done.13), channel_id=1, source_target_pairs={{0,15},{1,0},{2,1},{3,2},{4,3},{5,4},{6,5},{7,6},{8,7},{9,8},{10,9... | collective-permute-start | bytes 1572872 | tf_op jit(solution)/shard_map/ppermute | solution.py:109
  190.5 4.7 %collective-permute-start.15 = (bf16[1,128,512]{2,1,0:T(8,128)(2,1)S(1)}, bf16[1,128,512]{2,1,0:T(8,128)(2,1)S(1)}, u32[]{:S(2)}, u32[]{:S(2)}) collective-permute-start(bf16[1,128,512]{2,1,0:T(8,128)(2,1)S(1)} %get-tuple-element.17), channel_id=1, source_target_pairs={{0,1},{1,2},{2,3},{3,4},{4,5},{5,6},{6,7},{7,8},{8,9},{9,10},{10,1... | collective-permute-start | bytes 393224 | tf_op jit(solution)/shard_map/ppermute | solution.py:38
  193.3 6.3 %collective-permute-start.16 = (bf16[1,128,512]{2,1,0:T(8,128)(2,1)S(1)}, bf16[1,128,512]{2,1,0:T(8,128)(2,1)S(1)}, u32[]{:S(2)}, u32[]{:S(2)}) collective-permute-start(bf16[1,128,512]{2,1,0:T(8,128)(2,1)S(1)} %get-tuple-element.18), channel_id=1, source_target_pairs={{1,0},{2,1},{3,2},{4,3},{5,4},{6,5},{7,6},{8,7},{9,8},{10,9},{11,1... | collective-permute-start | bytes 393224 | tf_op jit(solution)/shard_map/ppermute | solution.py:40
  (14 other events, 221.8 us)
